TPU v7x, 32 devices: a whole 2x2x4 slice. The times are simulated.
32 devices in a mesh: twist: 4 (over y, x), walk: 8 (over z, core).
Axes of the slice: x: 2, y: 2, z: 4, core: 2. Of those that a mesh axis runs over, the one named last changes fastest.
Arguments:
- positions: float32 [2048, 3, 128], P(('twist', 'walk')), parts along dimension 0, may hold values from 0 to 25.1327
- inverse_slater: float32 [2048, 64, 128], P(('twist', 'walk')), parts along dimension 0, may hold values from -0.75 to 0.75
- orbitals: float32 [8, 64, 1536], P('twist'), parts along dimension 0, may hold values from -0.109375 to 0.109375
- twist_angle: float32 [12], P('twist'), parts along dimension 0, may hold values from -0.125 to 0.125
- trial_energy: float32 [4], P('twist'), parts along dimension 0, may hold values from 2 to 8
- multiplicity: int32 [2048], P(('twist', 'walk')), parts along dimension 0, may hold values from 1 to 3
- anchor_device: int32 [2048, 1], P(('twist', 'walk')), parts along dimension 0, may hold values from 0 to 7; in each aligned block of 64 rows (0 to 63, 64 to 127, ...) at most 16 rows name the same one
- anchor_slot: int32 [2048], P(('twist', 'walk')), parts along dimension 0, may hold values from 0 to 63
- live_count: int32 [32], P(('twist', 'walk')), parts along dimension 0, may hold values from 32 to 64, as said below
Outputs:
- new_inverse: float32 [2048, 64, 128], P(('twist', 'walk')), parts along dimension 0
- new_positions: float32 [2048, 3, 128], P(('twist', 'walk')), parts along dimension 0
- walker_scalars: float32 [2, 2048], P(None, ('twist', 'walk')), parts along dimension 1
- group_stats: float32 [8], P('twist'), parts along dimension 0
There are 4 independent parts, one for each index of `twist`. A program takes and returns all parts, laid end to end along the dimension named above; each array names one. Nothing has to cross between parts.
Inputs may be any that keep to these rules, and one draw needn't show every extreme that they name: `anchor_device`: within each device's 64 slots (its aligned block) no source device is named more than 16 times; in every draw some device names one source exactly 16 times. Slots of device d below live_count[d] are live, the rest empty; in every draw some device has all 64 slots live.
All inputs are finite; a program needn't handle non-finite values.
Results may differ from a plain program's by a relative error of at most 0.0004.
Values sent between devices are 32-bit elements; how exact they have to be, the bound alone decides.
A program may use at most 64 MiB of HBM per device.

v0:
```python
import math

import jax
import jax.numpy as jnp
from jax import lax
from jax.sharding import PartitionSpec as P

time_step = 0.1


def wave_momenta(twist_angle, plane_count):
    wave_index = jnp.arange(plane_count, dtype=jnp.int32)
    integer_grid = jnp.stack(
        [wave_index // 64 - plane_count // 128, wave_index // 8 % 8 - 4, wave_index % 8 - 4], axis=1
    )
    return twist_angle[None, :] + 0.25 * integer_grid.astype(jnp.float32)


def build_table(orbitals, momenta):
    cosine_part = orbitals[0]
    sine_part = orbitals[1]
    square_norm = (
        momenta[:, 0] * momenta[:, 0]
        + momenta[:, 1] * momenta[:, 1]
        + momenta[:, 2] * momenta[:, 2]
    )
    pieces = [jnp.concatenate([cosine_part, sine_part], axis=1)]
    for axis_id in range(3):
        component = momenta[:, axis_id][None, :]
        pieces.append(jnp.concatenate([component * sine_part, -component * cosine_part], axis=1))
    pieces.append(
        jnp.concatenate(
            [-square_norm[None, :] * cosine_part, -square_norm[None, :] * sine_part], axis=1
        )
    )
    return jnp.concatenate(pieces, axis=0).astype(jnp.bfloat16)


def plane_basis(momenta, position_block):
    phase_angle = (
        momenta[:, 0][None, :, None] * position_block[:, 0][:, None, :]
        + momenta[:, 1][None, :, None] * position_block[:, 1][:, None, :]
        + momenta[:, 2][None, :, None] * position_block[:, 2][:, None, :]
    )
    return jnp.concatenate([jnp.cos(phase_angle), jnp.sin(phase_angle)], axis=1).astype(
        jnp.bfloat16
    )


def pair_terms(position_block):
    offset = position_block[:, :, :, None] - position_block[:, :, None, :]
    square = offset[:, 0] * offset[:, 0] + offset[:, 1] * offset[:, 1] + offset[:, 2] * offset[:, 2]
    electrons = position_block.shape[2]
    labels = jnp.arange(electrons, dtype=jnp.int32)
    off_diag = (labels[:, None] != labels[None, :]).astype(jnp.float32)
    reciprocal = 1.0 / (9.0 + square)
    pair_grad = 54.0 * reciprocal * reciprocal * off_diag
    jastrow_grad = jnp.sum(pair_grad[:, None] * offset, axis=3)
    jastrow_lap = jnp.sum(
        off_diag
        * (162.0 * reciprocal * reciprocal - 216.0 * square * reciprocal * reciprocal * reciprocal),
        axis=2,
    )
    potential = 0.5 * jnp.sum(off_diag / jnp.sqrt(1.0 + square), axis=(1, 2))
    return (jastrow_grad, jastrow_lap, potential)


def walker_energy(values, inverse_block, position_block):
    walkers = inverse_block.shape[0]
    orbital_count = inverse_block.shape[1]
    electrons = inverse_block.shape[2]
    orbital = values[:, :orbital_count]
    gradients = values[:, orbital_count : 4 * orbital_count].reshape(
        walkers, 3, orbital_count, electrons
    )
    laplacian = values[:, 4 * orbital_count :]
    det_ratio = jnp.sum(orbital * inverse_block, axis=1)
    det_grad = jnp.sum(gradients * inverse_block[:, None], axis=2)
    det_lap = jnp.sum(laplacian * inverse_block, axis=1)
    jastrow_grad, jastrow_lap, potential = pair_terms(position_block)
    cross_term = (
        det_grad[:, 0] * jastrow_grad[:, 0]
        + det_grad[:, 1] * jastrow_grad[:, 1]
        + det_grad[:, 2] * jastrow_grad[:, 2]
    )
    jastrow_square = (
        jastrow_grad[:, 0] * jastrow_grad[:, 0]
        + jastrow_grad[:, 1] * jastrow_grad[:, 1]
        + jastrow_grad[:, 2] * jastrow_grad[:, 2]
    )
    kinetic = (
        det_ratio * det_lap
        + 2.0 * det_ratio * cross_term
        + det_ratio * det_ratio * (jastrow_square + jastrow_lap)
    ) / (1.0 + det_ratio * det_ratio)
    return (potential - 0.5 * jnp.sum(kinetic, axis=1)) / electrons


def block_energy(coef_table, momenta, inverse_block, position_block):
    basis_block = plane_basis(momenta, position_block)
    values = jnp.einsum("cg,bgk->bck", coef_table, basis_block, preferred_element_type=jnp.float32)
    return walker_energy(values, inverse_block, position_block)


def local_energies(coef_table, momenta, inverse_slater, positions):
    walk_dev = positions.shape[0]
    orbital_count = inverse_slater.shape[1]
    electrons = inverse_slater.shape[2]
    group = math.gcd(8, walk_dev)
    inverse_blocks = inverse_slater.reshape(walk_dev // group, group, orbital_count, electrons)
    position_blocks = positions.reshape(walk_dev // group, group, 3, electrons)
    energy = lax.map(
        lambda blocks: block_energy(coef_table, momenta, blocks[0], blocks[1]),
        (inverse_blocks, position_blocks),
    )
    return energy.reshape(walk_dev)


def build_requests(source_device, slot_rank, wanted, peer_count, capacity):
    peer_ids = jnp.arange(peer_count, dtype=jnp.int32)
    room_ids = jnp.arange(capacity, dtype=jnp.int32)
    matches = (source_device[None, None, :] == peer_ids[:, None, None]) & (
        slot_rank[None, None, :] == room_ids[None, :, None]
    )
    return jnp.sum(jnp.where(matches, wanted[None, None, :], 0), axis=2)


def body(
    positions,
    inverse_slater,
    orbitals,
    twist_angle,
    trial_energy,
    multiplicity,
    anchor_device,
    anchor_slot,
    live_count,
):
    walk_dev = positions.shape[0]
    orbital_count = inverse_slater.shape[1]
    electrons = inverse_slater.shape[2]
    peer_count = lax.axis_size("walk")
    capacity = min(walk_dev, max(2, 2 * walk_dev // peer_count))
    slot_ids = jnp.arange(walk_dev, dtype=jnp.int32)
    source_device = anchor_device[:, 0]
    same_source = (source_device[:, None] == source_device[None, :]) & (
        slot_ids[None, :] < slot_ids[:, None]
    )
    slot_rank = jnp.sum(same_source.astype(jnp.int32), axis=1)
    requests = build_requests(source_device, slot_rank, anchor_slot, peer_count, capacity)
    served = lax.all_to_all(requests, "walk", split_axis=0, concat_axis=0, tiled=True)
    served_flat = served.reshape(peer_count * capacity)
    send_inverse = jnp.take(inverse_slater, served_flat, axis=0).reshape(
        peer_count, capacity, orbital_count, electrons
    )
    send_positions = jnp.take(positions, served_flat, axis=0).reshape(
        peer_count, capacity, 3, electrons
    )
    recv_inverse, recv_positions = (
        lax.all_to_all(send_inverse, "walk", split_axis=0, concat_axis=0, tiled=True),
        lax.all_to_all(send_positions, "walk", split_axis=0, concat_axis=0, tiled=True),
    )
    momenta = wave_momenta(twist_angle, orbitals.shape[2])
    coef_table = build_table(orbitals, momenta)
    energy = local_energies(coef_table, momenta, inverse_slater, positions)
    weight = jnp.exp(-time_step * (energy - trial_energy[0]))
    scaled = multiplicity.astype(jnp.float32) * weight
    totals = lax.psum((jnp.sum(scaled * energy), jnp.sum(scaled)), "walk")
    group_stats = jnp.stack([totals[0], totals[1]]) / (walk_dev * peer_count)
    send_scalars = (
        jnp.take(jnp.stack([weight, energy]), served_flat, axis=1)
        .reshape(2, peer_count, capacity)
        .transpose(1, 0, 2)
    )
    recv_scalars = lax.all_to_all(send_scalars, "walk", split_axis=0, concat_axis=0, tiled=True)
    target = source_device * capacity + slot_rank
    live_slot = slot_ids < live_count[0]
    new_inverse = jnp.where(
        live_slot[:, None, None],
        jnp.take(
            recv_inverse.reshape(peer_count * capacity, orbital_count, electrons), target, axis=0
        ),
        0.0,
    )
    new_positions = jnp.where(
        live_slot[:, None, None],
        jnp.take(recv_positions.reshape(peer_count * capacity, 3, electrons), target, axis=0),
        0.0,
    )
    carried = jnp.take(
        recv_scalars.transpose(1, 0, 2).reshape(2, peer_count * capacity), target, axis=1
    )
    walker_scalars = jnp.where(live_slot[None, :], carried, 0.0)
    return (new_inverse, new_positions, walker_scalars, group_stats)


def solution(mesh):
    in_specs = (
        P(("twist", "walk"), None, None),
        P(("twist", "walk"), None, None),
        P("twist", None, None),
        P("twist"),
        P("twist"),
        P(("twist", "walk")),
        P(("twist", "walk"), None),
        P(("twist", "walk")),
        P(("twist", "walk")),
    )
    out_specs = (
        P(("twist", "walk"), None, None),
        P(("twist", "walk"), None, None),
        P(None, ("twist", "walk")),
        P("twist"),
    )
    return jax.shard_map(body, mesh=mesh, in_specs=in_specs, out_specs=out_specs, check_vma=False)
```

profile of v0, /device:TPU:20, one launch (start us, length us, event | category | flops | bytes accessed | tf_op | source)
XLA Modules:
  0.0 387.5 jit_solution(11845040570823548435)
XLA Ops:
  0.6 0.9 convert_reduce_fusion
  1.6 0.7 iota_compare_fusion.3
  2.2 1.5 select_reduce_fusion
  3.7 5.2 %all-to-all-start = ((s32[8,1,16]{2,1,0:T(1,128)}), s32[8,1,16]{2,1,0:T(1,128)S(1)}, u32[]{:S(2)}, u32[]{:S(2)}) async-start(s32[8,1,16]{2,1,0:T(1,128)} %bitcast.20), calls=%async_computation | async-start | bytes 8192 | tf_op jit(solution)/shard_map/all_to_all | solution.py:151
  9.0 0.7 fusion.37
  9.8 1.2 bitcast_convert_fusion.1
  11.4 1.3 copy-done.3
  12.7 0.9 copy-done.1
  13.6 233.7 %while.10 = (s32[]{:T(128)}, f32[8,8]{1,0:T(8,128)S(1)}, f32[8,8,3,128]{3,1,0,2:T(8,128)S(1)}, f32[1536,3]{0,1:T(4,128)S(1)}, bf16[320,3072]{1,0:T(8,128)(2,1)},...) while((s32[]{:T(128)}, f32[8,8]{1,0:T(8,128)S(1)}, f32[8,8,3,128]{3,1,0,2:T(8,128)S(1)}, ...), condition=%wide.region_10.11_spmd, body=%wide.region_2.10_spmd.sunk | while | flops 2042277888 | bytes 33073500 | solution.py:112
  13.6 24.5 %cosine_convert_fusion.2 = (bf16[8,1536,128]{2,1,0:T(8,128)(2,1)S(1)}, bf16[8,1536,128]{2,1,0:T(8,128)(2,1)S(1)}) fusion(f32[8,128]{1,0:T(8,128)S(1)} %get-tuple-element.193, f32[1536]{0:T(1024)S(1)} %get-tuple-element.194, f32[8,128]{1,0:T(8,128)S(1)} %get-tuple-element.195, f32[1536]{0:T(1024)S(1)} %get-tuple-element.196, ...), kind=kLoop, calls=%fused_computation.11.clone.1 | loop fusion | flops 11010048 | bytes 6322176 | tf_op jit(solution)/shard_map/convert
  38.1 2.2 fusion.59
  41.3 0.9 multiply_reduce_fusion.6
  42.9 24.5 %cosine_convert_fusion.2 = (bf16[8,1536,128]{2,1,0:T(8,128)(2,1)S(1)}, bf16[8,1536,128]{2,1,0:T(8,128)(2,1)S(1)}) fusion(f32[8,128]{1,0:T(8,128)S(1)} %get-tuple-element.193, f32[1536]{0:T(1024)S(1)} %get-tuple-element.194, f32[8,128]{1,0:T(8,128)S(1)} %get-tuple-element.195, f32[1536]{0:T(1024)S(1)} %get-tuple-element.196, ...), kind=kLoop, calls=%fused_computation.11.clone.1 | loop fusion | flops 11010048 | bytes 6322176 | tf_op jit(solution)/shard_map/convert
  67.4 2.2 fusion.59
  70.5 0.9 multiply_reduce_fusion.6
  72.1 24.5 %cosine_convert_fusion.2 = (bf16[8,1536,128]{2,1,0:T(8,128)(2,1)S(1)}, bf16[8,1536,128]{2,1,0:T(8,128)(2,1)S(1)}) fusion(f32[8,128]{1,0:T(8,128)S(1)} %get-tuple-element.193, f32[1536]{0:T(1024)S(1)} %get-tuple-element.194, f32[8,128]{1,0:T(8,128)S(1)} %get-tuple-element.195, f32[1536]{0:T(1024)S(1)} %get-tuple-element.196, ...), kind=kLoop, calls=%fused_computation.11.clone.1 | loop fusion | flops 11010048 | bytes 6322176 | tf_op jit(solution)/shard_map/convert
  96.6 2.2 fusion.59
  99.7 0.9 multiply_reduce_fusion.6
  101.3 24.5 %cosine_convert_fusion.2 = (bf16[8,1536,128]{2,1,0:T(8,128)(2,1)S(1)}, bf16[8,1536,128]{2,1,0:T(8,128)(2,1)S(1)}) fusion(f32[8,128]{1,0:T(8,128)S(1)} %get-tuple-element.193, f32[1536]{0:T(1024)S(1)} %get-tuple-element.194, f32[8,128]{1,0:T(8,128)S(1)} %get-tuple-element.195, f32[1536]{0:T(1024)S(1)} %get-tuple-element.196, ...), kind=kLoop, calls=%fused_computation.11.clone.1 | loop fusion | flops 11010048 | bytes 6322176 | tf_op jit(solution)/shard_map/convert
  125.8 2.2 fusion.59
  128.9 0.9 multiply_reduce_fusion.6
  130.5 24.5 %cosine_convert_fusion.2 = (bf16[8,1536,128]{2,1,0:T(8,128)(2,1)S(1)}, bf16[8,1536,128]{2,1,0:T(8,128)(2,1)S(1)}) fusion(f32[8,128]{1,0:T(8,128)S(1)} %get-tuple-element.193, f32[1536]{0:T(1024)S(1)} %get-tuple-element.194, f32[8,128]{1,0:T(8,128)S(1)} %get-tuple-element.195, f32[1536]{0:T(1024)S(1)} %get-tuple-element.196, ...), kind=kLoop, calls=%fused_computation.11.clone.1 | loop fusion | flops 11010048 | bytes 6322176 | tf_op jit(solution)/shard_map/convert
  155.0 2.2 fusion.59
  158.2 0.9 multiply_reduce_fusion.6
  159.7 24.5 %cosine_convert_fusion.2 = (bf16[8,1536,128]{2,1,0:T(8,128)(2,1)S(1)}, bf16[8,1536,128]{2,1,0:T(8,128)(2,1)S(1)}) fusion(f32[8,128]{1,0:T(8,128)S(1)} %get-tuple-element.193, f32[1536]{0:T(1024)S(1)} %get-tuple-element.194, f32[8,128]{1,0:T(8,128)S(1)} %get-tuple-element.195, f32[1536]{0:T(1024)S(1)} %get-tuple-element.196, ...), kind=kLoop, calls=%fused_computation.11.clone.1 | loop fusion | flops 11010048 | bytes 6322176 | tf_op jit(solution)/shard_map/convert
  184.2 2.2 fusion.59
  187.4 0.9 multiply_reduce_fusion.6
  188.9 24.5 %cosine_convert_fusion.2 = (bf16[8,1536,128]{2,1,0:T(8,128)(2,1)S(1)}, bf16[8,1536,128]{2,1,0:T(8,128)(2,1)S(1)}) fusion(f32[8,128]{1,0:T(8,128)S(1)} %get-tuple-element.193, f32[1536]{0:T(1024)S(1)} %get-tuple-element.194, f32[8,128]{1,0:T(8,128)S(1)} %get-tuple-element.195, f32[1536]{0:T(1024)S(1)} %get-tuple-element.196, ...), kind=kLoop, calls=%fused_computation.11.clone.1 | loop fusion | flops 11010048 | bytes 6322176 | tf_op jit(solution)/shard_map/convert
  213.4 2.2 fusion.59
  216.6 0.9 multiply_reduce_fusion.6
  218.2 24.5 %cosine_convert_fusion.2 = (bf16[8,1536,128]{2,1,0:T(8,128)(2,1)S(1)}, bf16[8,1536,128]{2,1,0:T(8,128)(2,1)S(1)}) fusion(f32[8,128]{1,0:T(8,128)S(1)} %get-tuple-element.193, f32[1536]{0:T(1024)S(1)} %get-tuple-element.194, f32[8,128]{1,0:T(8,128)S(1)} %get-tuple-element.195, f32[1536]{0:T(1024)S(1)} %get-tuple-element.196, ...), kind=kLoop, calls=%fused_computation.11.clone.1 | loop fusion | flops 11010048 | bytes 6322176 | tf_op jit(solution)/shard_map/convert
  242.7 2.2 fusion.59
  245.8 0.9 multiply_reduce_fusion.6
  248.6 0.7 reduce.15
  249.4 0.9 gather_fusion.2
  251.7 5.1 %all-to-all-start.3 = ((f32[8,2,16]{2,1,0:T(2,128)}), f32[8,2,16]{2,1,0:T(2,128)S(1)}, u32[]{:S(2)}, u32[]{:S(2)}) async-start(f32[8,2,16]{2,1,0:T(2,128)} %select_bitcast_fusion.1), calls=%async_computation.3 | async-start | bytes 16384 | tf_op jit(solution)/shard_map/all_to_all | solution.py:175
  256.8 0.8 copy_select_fusion
  257.5 2.8 gather_fusion
  260.3 5.4 %all-to-all-start.2 = ((f32[8,16,3,128]{3,1,2,0:T(8,128)}), f32[8,16,3,128]{3,1,2,0:T(8,128)S(1)}, u32[]{:S(2)}, u32[]{:S(2)}) async-start(f32[8,16,3,128]{3,1,2,0:T(8,128)} %copy_select_fusion), calls=%async_computation.2 | async-start | bytes 393216 | tf_op jit(solution)/shard_map/all_to_all | solution.py:161
  265.7 4.5 %broadcast_select_fusion = f32[8,16,64,128]{3,2,1,0:T(8,128)} fusion(f32[8,16,64,128]{3,2,1,0:T(8,128)} %bitcast.148, pred[8,16]{1,0:T(8,128)(4,1)S(1)} %compare_and_fusion), kind=kLoop, calls=%fused_computation.58 | loop fusion | flops 1048576 | bytes 8388736 | tf_op jit(solution)/shard_map/jit(_take)/select_n | solution.py:153
  270.2 0.7 all-to-all-done.2
  270.9 7.6 %all-to-all-start.1 = ((f32[8,16,64,128]{3,2,1,0:T(8,128)}), f32[8,16,64,128]{3,2,1,0:T(8,128)}, u32[]{:S(2)}, u32[]{:S(2)}) async-start(f32[8,16,64,128]{3,2,1,0:T(8,128)} %broadcast_select_fusion), calls=%async_computation.1 | async-start | bytes 8388608 | tf_op jit(solution)/shard_map/all_to_all | solution.py:160
  279.2 98.2 %all-reduce = (f32[1]{0:T(128)}, f32[1]{0:T(128)}) all-reduce(f32[1]{0:T(128)} %bitcast.40, f32[1]{0:T(128)} %bitcast.39), channel_id=1, replica_groups=mesh['twist'=4,'walk'=8] {'walk'}, use_global_device_ids=true, to_apply=%region_14.15 | all-reduce | flops 2 | bytes 16 | tf_op jit(solution)/shard_map/psum | solution.py:168
  378.0 1.9 maximum_multiply_fusion
  381.5 0.7 gather_fusion.3
  382.4 0.6 copy.58
  383.0 2.9 gather_fusion.1
  385.9 1.6 select_select_fusion
  (176 shorter events, 17.0 us)
Async XLA Ops:
  0.6 10.3 %copy-start.2 = (f32[2,64,1536]{2,1,0:T(8,128)S(1)}, f32[2,64,1536]{2,1,0:T(8,128)}, u32[]{:S(2)}) copy-start(f32[2,64,1536]{2,1,0:T(8,128)} %param.13) | copy-start | bytes 2359300
  3.7 244.4 %all-to-all-start = ((s32[8,1,16]{2,1,0:T(1,128)}), s32[8,1,16]{2,1,0:T(1,128)S(1)}, u32[]{:S(2)}, u32[]{:S(2)}) async-start(s32[8,1,16]{2,1,0:T(1,128)} %bitcast.20), calls=%async_computation | async-start | bytes 8192 | tf_op jit(solution)/shard_map/all_to_all | solution.py:151
  11.2 1.4 copy-start
  11.2 2.4 copy-start.1
  11.4 1.3 copy-start.3
  13.6 24.5 %copy-start.4 = (bf16[320,3072]{1,0:T(8,128)(2,1)S(1)}, bf16[320,3072]{1,0:T(8,128)(2,1)}, u32[]{:S(2)}) copy-start(bf16[320,3072]{1,0:T(8,128)(2,1)} %get-tuple-element.229) | copy-start | bytes 5898244 | tf_op jit(solution)/shard_map/while
  42.9 24.5 %copy-start.4 = (bf16[320,3072]{1,0:T(8,128)(2,1)S(1)}, bf16[320,3072]{1,0:T(8,128)(2,1)}, u32[]{:S(2)}) copy-start(bf16[320,3072]{1,0:T(8,128)(2,1)} %get-tuple-element.229) | copy-start | bytes 5898244 | tf_op jit(solution)/shard_map/while
  72.1 24.5 %copy-start.4 = (bf16[320,3072]{1,0:T(8,128)(2,1)S(1)}, bf16[320,3072]{1,0:T(8,128)(2,1)}, u32[]{:S(2)}) copy-start(bf16[320,3072]{1,0:T(8,128)(2,1)} %get-tuple-element.229) | copy-start | bytes 5898244 | tf_op jit(solution)/shard_map/while
  101.3 24.5 %copy-start.4 = (bf16[320,3072]{1,0:T(8,128)(2,1)S(1)}, bf16[320,3072]{1,0:T(8,128)(2,1)}, u32[]{:S(2)}) copy-start(bf16[320,3072]{1,0:T(8,128)(2,1)} %get-tuple-element.229) | copy-start | bytes 5898244 | tf_op jit(solution)/shard_map/while
  130.5 24.5 %copy-start.4 = (bf16[320,3072]{1,0:T(8,128)(2,1)S(1)}, bf16[320,3072]{1,0:T(8,128)(2,1)}, u32[]{:S(2)}) copy-start(bf16[320,3072]{1,0:T(8,128)(2,1)} %get-tuple-element.229) | copy-start | bytes 5898244 | tf_op jit(solution)/shard_map/while
  159.7 24.5 %copy-start.4 = (bf16[320,3072]{1,0:T(8,128)(2,1)S(1)}, bf16[320,3072]{1,0:T(8,128)(2,1)}, u32[]{:S(2)}) copy-start(bf16[320,3072]{1,0:T(8,128)(2,1)} %get-tuple-element.229) | copy-start | bytes 5898244 | tf_op jit(solution)/shard_map/while
  188.9 24.5 %copy-start.4 = (bf16[320,3072]{1,0:T(8,128)(2,1)S(1)}, bf16[320,3072]{1,0:T(8,128)(2,1)}, u32[]{:S(2)}) copy-start(bf16[320,3072]{1,0:T(8,128)(2,1)} %get-tuple-element.229) | copy-start | bytes 5898244 | tf_op jit(solution)/shard_map/while
  218.2 24.5 %copy-start.4 = (bf16[320,3072]{1,0:T(8,128)(2,1)S(1)}, bf16[320,3072]{1,0:T(8,128)(2,1)}, u32[]{:S(2)}) copy-start(bf16[320,3072]{1,0:T(8,128)(2,1)} %get-tuple-element.229) | copy-start | bytes 5898244 | tf_op jit(solution)/shard_map/while
  251.7 8.6 %all-to-all-start.3 = ((f32[8,2,16]{2,1,0:T(2,128)}), f32[8,2,16]{2,1,0:T(2,128)S(1)}, u32[]{:S(2)}, u32[]{:S(2)}) async-start(f32[8,2,16]{2,1,0:T(2,128)} %select_bitcast_fusion.1), calls=%async_computation.3 | async-start | bytes 16384 | tf_op jit(solution)/shard_map/all_to_all | solution.py:175
  260.3 10.6 %all-to-all-start.2 = ((f32[8,16,3,128]{3,1,2,0:T(8,128)}), f32[8,16,3,128]{3,1,2,0:T(8,128)S(1)}, u32[]{:S(2)}, u32[]{:S(2)}) async-start(f32[8,16,3,128]{3,1,2,0:T(8,128)} %copy_select_fusion), calls=%async_computation.2 | async-start | bytes 393216 | tf_op jit(solution)/shard_map/all_to_all | solution.py:161
  270.2 8.4 %copy-start.5 = (s32[64]{0:T(128)S(1)}, s32[64]{0:T(128)}, u32[]{:S(2)}) copy-start(s32[64]{0:T(128)} %param.16) | copy-start | bytes 772
  270.2 109.7 %copy-start.6 = (s32[64,1]{0,1:T(1,128)S(1)}, s32[64,1]{0,1:T(1,128)}, u32[]{:S(2)}) copy-start(s32[64,1]{0,1:T(1,128)} %param.17) | copy-start | bytes 772
  270.9 112.1 %all-to-all-start.1 = ((f32[8,16,64,128]{3,2,1,0:T(8,128)}), f32[8,16,64,128]{3,2,1,0:T(8,128)}, u32[]{:S(2)}, u32[]{:S(2)}) async-start(f32[8,16,64,128]{3,2,1,0:T(8,128)} %broadcast_select_fusion), calls=%async_computation.1 | async-start | bytes 8388608 | tf_op jit(solution)/shard_map/all_to_all | solution.py:160
where the time goes:
time: 388 us; the launch traced here: 387 us
  other arithmetic  229 us (59%)
  blocking collectives  98.2 us (25%)
  starting transfers between devices  23.3 us (6%)
  matrix products  17.6 us (5%)
  local copies, waits for them, and re-layouts  15.6 us (4%)
    another operation x9, other arithmetic  196 us
    psum x1, blocking collectives, body(): totals = lax.psum((jnp.sum(scaled * energy), jnp.sum(scaled)), 'walk')  98.2 us
    dot_general x8, matrix products, block_energy(): jnp.einsum('cg,bgk->bck', coef_table, basis_block, preferred_element_type...  17.6 us
  transfers between devices with their start and end apart: 4, of which 1 were waited for; matrix products, arithmetic and copies ran while one was open for 64% of the time, Pallas kernels for 0%

commit v1 on v0

v1 whole, which is shorter than its diff:
```python
import jax
import jax.numpy as jnp
import numpy as np
from jax import lax
from jax.experimental import pallas as pl
from jax.experimental.pallas import tpu as pltpu
from jax.sharding import PartitionSpec as P

time_step = 0.1
side = 8


def wave_momenta(twist_angle, plane_count):
    wave_index = jnp.arange(plane_count, dtype=jnp.int32)
    integer_grid = jnp.stack(
        [wave_index // 64 - plane_count // 128, wave_index // 8 % 8 - 4, wave_index % 8 - 4], axis=1
    )
    return twist_angle[None, :] + 0.25 * integer_grid.astype(jnp.float32)


def build_table(orbitals, momenta):
    cosine_part = orbitals[0]
    sine_part = orbitals[1]
    square_norm = (
        momenta[:, 0] * momenta[:, 0]
        + momenta[:, 1] * momenta[:, 1]
        + momenta[:, 2] * momenta[:, 2]
    )
    pieces = [jnp.concatenate([cosine_part, sine_part], axis=1)]
    for axis_id in range(3):
        component = momenta[:, axis_id][None, :]
        pieces.append(jnp.concatenate([component * sine_part, -component * cosine_part], axis=1))
    pieces.append(
        jnp.concatenate(
            [-square_norm[None, :] * cosine_part, -square_norm[None, :] * sine_part], axis=1
        )
    )
    return jnp.concatenate(pieces, axis=0).astype(jnp.bfloat16)


def axis_waves(momenta, coordinate):
    angle = momenta[None, :, None] * coordinate[:, None, :]
    return jnp.concatenate([jnp.cos(angle), jnp.sin(angle)], axis=1)


def energy_kernel(
    table_ref, inverse_ref, x_ref, yz_ref, pos_ref, column_ref, out_ref, basis, product, det, pair
):
    group, orbital_count, electrons = inverse_ref.shape
    depth = x_ref.shape[1] // 2
    area = side * side
    planes = depth * area
    for w in range(group):
        cols = slice(w * electrons, (w + 1) * electrons)
        cy, sy, cz, sz = [yz_ref[w, k * side : (k + 1) * side, :] for k in range(4)]

        def outer(a, b):
            return (a[:, None, :] * b[None, :, :]).reshape(area, electrons)

        cyz = outer(cy, cz) - outer(sy, sz)
        syz = outer(sy, cz) + outer(cy, sz)
        for g in range(depth):
            cx, sx = x_ref[w, g : g + 1, :], x_ref[w, depth + g : depth + g + 1, :]
            basis[g * area : (g + 1) * area, cols] = (cx * cyz - sx * syz).astype(jnp.bfloat16)
            basis[planes + g * area : planes + (g + 1) * area, cols] = (
                sx * cyz + cx * syz
            ).astype(jnp.bfloat16)
    product[...] = jnp.dot(table_ref[...], basis[...], preferred_element_type=jnp.float32)
    for w in range(group):
        cols = slice(w * electrons, (w + 1) * electrons)
        inverse = inverse_ref[w]
        for k in range(5):
            block = product[k * orbital_count : (k + 1) * orbital_count, cols]
            det[k, w : w + 1, :] = jnp.sum(block * inverse, axis=0, keepdims=True)
        chunk = 32
        sums = [jnp.zeros((chunk, electrons), jnp.float32) for _ in range(5)]
        here = [jnp.broadcast_to(pos_ref[w, a : a + 1, :], (chunk, electrons)) for a in range(3)]
        for first in range(0, electrons, chunk):
            offs = [
                here[a] - column_ref[w, first : first + chunk, a : a + 1] for a in range(3)
            ]
            square = offs[0] * offs[0] + offs[1] * offs[1] + offs[2] * offs[2]
            inv = 1.0 / (9.0 + square)
            inv2 = inv * inv
            for a in range(3):
                sums[a] = sums[a] + inv2 * offs[a]
            sums[3] = sums[3] + inv2 * (1944.0 * inv - 54.0)
            sums[4] = sums[4] + lax.rsqrt(1.0 + square)
        for k in range(5):
            pair[k, w : w + 1, :] = jnp.sum(sums[k], axis=0, keepdims=True)
    ratio, lap = det[0], det[4]
    jas = [54.0 * pair[a] for a in range(3)]
    cross = det[1] * jas[0] + det[2] * jas[1] + det[3] * jas[2]
    jas_square = jas[0] * jas[0] + jas[1] * jas[1] + jas[2] * jas[2]
    jas_lap = pair[3] - 2.0
    kinetic = (
        ratio * lap + 2.0 * ratio * cross + ratio * ratio * (jas_square + jas_lap)
    ) / (1.0 + ratio * ratio)
    out_ref[...] = 0.5 * ((pair[4] - 1.0) - kinetic)


def local_energies(table, momenta, inverse_slater, positions):
    walkers, orbital_count, electrons = inverse_slater.shape
    group = 8
    area = side * side
    planes = momenta.shape[0]
    x_rows = axis_waves(momenta[::area, 0], positions[:, 0])
    yz_rows = jnp.concatenate(
        [
            axis_waves(momenta[:area:side, 1], positions[:, 1]),
            axis_waves(momenta[:side, 2], positions[:, 2]),
        ],
        axis=1,
    )
    column = positions.transpose(0, 2, 1)

    def block(*shape):
        return pl.BlockSpec((group,) + shape, lambda i: (i,) + (0,) * len(shape))

    rows = pl.pallas_call(
        energy_kernel,
        out_shape=jax.ShapeDtypeStruct((walkers, electrons), jnp.float32),
        grid=(walkers // group,),
        in_specs=[
            pl.BlockSpec(table.shape, lambda i: (0, 0)),
            block(orbital_count, electrons),
            block(x_rows.shape[1], electrons),
            block(yz_rows.shape[1], electrons),
            block(3, electrons),
            block(electrons, 3),
        ],
        out_specs=block(electrons),
        scratch_shapes=[
            pltpu.VMEM((2 * planes, group * electrons), jnp.bfloat16),
            pltpu.VMEM((5 * orbital_count, group * electrons), jnp.float32),
            pltpu.VMEM((5, group, electrons), jnp.float32),
            pltpu.VMEM((5, group, electrons), jnp.float32),
        ],
        compiler_params=pltpu.CompilerParams(vmem_limit_bytes=40 * 1024 * 1024),
        cost_estimate=pl.CostEstimate(
            flops=2 * 5 * orbital_count * 2 * planes * walkers * electrons * 2,
            bytes_accessed=walkers * orbital_count * electrons * 4,
            transcendentals=walkers * electrons * electrons * 2,
        ),
    )(table, inverse_slater, x_rows, yz_rows, positions, column)
    return jnp.sum(rows, axis=1) / electrons


def build_requests(source_device, slot_rank, wanted, peer_count, capacity):
    peer_ids = jnp.arange(peer_count, dtype=jnp.int32)
    room_ids = jnp.arange(capacity, dtype=jnp.int32)
    matches = (source_device[None, None, :] == peer_ids[:, None, None]) & (
        slot_rank[None, None, :] == room_ids[None, :, None]
    )
    return jnp.sum(jnp.where(matches, wanted[None, None, :], 0), axis=2)


def body(
    positions,
    inverse_slater,
    orbitals,
    twist_angle,
    trial_energy,
    multiplicity,
    anchor_device,
    anchor_slot,
    live_count,
):
    walk_dev = positions.shape[0]
    orbital_count = inverse_slater.shape[1]
    electrons = inverse_slater.shape[2]
    peer_count = lax.axis_size("walk")
    capacity = min(walk_dev, max(2, 2 * walk_dev // peer_count))
    slot_ids = jnp.arange(walk_dev, dtype=jnp.int32)
    source_device = anchor_device[:, 0]
    same_source = (source_device[:, None] == source_device[None, :]) & (
        slot_ids[None, :] < slot_ids[:, None]
    )
    slot_rank = jnp.sum(same_source.astype(jnp.int32), axis=1)
    requests = build_requests(source_device, slot_rank, anchor_slot, peer_count, capacity)
    served = lax.all_to_all(requests, "walk", split_axis=0, concat_axis=0, tiled=True)
    served_flat = served.reshape(peer_count * capacity)
    send_inverse = jnp.take(inverse_slater, served_flat, axis=0).reshape(
        peer_count, capacity, orbital_count, electrons
    )
    send_positions = jnp.take(positions, served_flat, axis=0).reshape(
        peer_count, capacity, 3, electrons
    )
    recv_inverse, recv_positions = (
        lax.all_to_all(send_inverse, "walk", split_axis=0, concat_axis=0, tiled=True),
        lax.all_to_all(send_positions, "walk", split_axis=0, concat_axis=0, tiled=True),
    )
    momenta = wave_momenta(twist_angle, orbitals.shape[2])
    table = build_table(orbitals, momenta)
    energy = local_energies(table, momenta, inverse_slater, positions)
    weight = jnp.exp(-time_step * (energy - trial_energy[0]))
    scaled = multiplicity.astype(jnp.float32) * weight
    shared = lax.all_gather(jnp.stack([weight, energy, scaled]), "walk")
    group_stats = jnp.stack(
        [jnp.sum(shared[:, 2] * shared[:, 1]), jnp.sum(shared[:, 2])]
    ) / (walk_dev * peer_count)
    target = source_device * capacity + slot_rank
    live_slot = slot_ids < live_count[0]
    new_inverse = jnp.where(
        live_slot[:, None, None],
        jnp.take(
            recv_inverse.reshape(peer_count * capacity, orbital_count, electrons), target, axis=0
        ),
        0.0,
    )
    new_positions = jnp.where(
        live_slot[:, None, None],
        jnp.take(recv_positions.reshape(peer_count * capacity, 3, electrons), target, axis=0),
        0.0,
    )
    source = source_device * walk_dev + anchor_slot
    carried = jnp.take(
        shared[:, :2].transpose(1, 0, 2).reshape(2, peer_count * walk_dev), source, axis=1
    )
    walker_scalars = jnp.where(live_slot[None, :], carried, 0.0)
    return (new_inverse, new_positions, walker_scalars, group_stats)


def solution(mesh):
    in_specs = (
        P(("twist", "walk"), None, None),
        P(("twist", "walk"), None, None),
        P("twist", None, None),
        P("twist"),
        P("twist"),
        P(("twist", "walk")),
        P(("twist", "walk"), None),
        P(("twist", "walk")),
        P(("twist", "walk")),
    )
    out_specs = (
        P(("twist", "walk"), None, None),
        P(("twist", "walk"), None, None),
        P(None, ("twist", "walk")),
        P("twist"),
    )
    return jax.shard_map(body, mesh=mesh, in_specs=in_specs, out_specs=out_specs, check_vma=False)
```

time: 388 us -> 159 us (0.41)
  the two profiles are of different devices: /device:TPU:20 before, /device:TPU:0 now
where the time goes in v1:
time: 159 us; the launch traced here: 158 us
  blocking collectives  59.7 us (38%)
  Pallas kernels  31.6 us (20%)
  other arithmetic  26.4 us (17%)
  local copies, waits for them, and re-layouts  18.3 us (12%)
  starting transfers between devices  16 us (10%)
  waiting for transfers between devices  3.82 us (2%)
  between operations  2.36 us (1%)
    all_gather x1, blocking collectives, body(): shared = lax.all_gather(jnp.stack([weight, energy, scaled]), 'walk')  59.7 us
    pallas_call x1, Pallas kernels, local_energies(): pl.pallas_call(energy_kernel, out_shape=jax.ShapeDtypeStruct((walkers, el...  31.6 us
    cos x3, other arithmetic, axis_waves(): return jnp.concatenate([jnp.cos(angle), jnp.sin(angle)], axis=1)  7.35 us
    unnamed x36, local copies, waits for them, and re-layouts  6.54 us
    all_to_all x1, starting transfers between devices, body(): lax.all_to_all(requests, 'walk', split_axis=0, concat_axis=0, tiled=True)  6.35 us
    all_to_all x1, starting transfers between devices, body(): lax.all_to_all(send_positions, 'walk', split_axis=0, concat_axis=0, tiled...  5.1 us
    all_to_all x1, starting transfers between devices, body(): lax.all_to_all(send_inverse, 'walk', split_axis=0, concat_axis=0, tiled=T...  4.56 us
    select_n x2, other arithmetic, body(): jnp.take(inverse_slater, served_flat, axis=0)  4.5 us
  transfers between devices with their start and end apart: 3, of which 1 were waited for; matrix products, arithmetic and copies ran while one was open for 18% of the time, Pallas kernels for 20%

profile of v1, /device:TPU:0, one launch (start us, length us, event | category | flops | bytes accessed | tf_op | source)
XLA Modules:
  0.0 158.2 jit_solution(17161406206734218928)
XLA Ops:
  0.7 0.9 convert_reduce_fusion
  1.6 0.7 iota_compare_fusion.2
  2.3 1.5 select_reduce_fusion
  3.8 6.4 %all-to-all-start = ((s32[8,1,16]{2,1,0:T(1,128)}), s32[8,1,16]{2,1,0:T(1,128)S(1)}, u32[]{:S(2)}, u32[]{:S(2)}) async-start(s32[8,1,16]{2,1,0:T(1,128)} %bitcast.5), calls=%async_computation | async-start | bytes 8192 | tf_op jit(solution)/shard_map/all_to_all | solution.py:181
  10.2 0.7 fusion.10
  10.9 0.1 slice_reduce_fusion
  10.9 0.1 slice.56
  11.0 0.1 slice.54
  11.2 1.9 %bitcast_convert_fusion.1 = (bf16[64,1536]{1,0:T(8,128)(2,1)}, bf16[64,1536]{1,0:T(8,128)(2,1)}) fusion(f32[2,64,1536]{2,1,0:T(8,128)} %param.11), kind=kLoop, calls=%fused_computation.29 | loop fusion | bytes 786432 | tf_op jit(solution)/shard_map/convert.13
  13.1 0.8 slice_bitcast_fusion.1
  13.9 1.7 %multiply_cosine_fusion.2 = (f32[64,8,128]{2,1,0:T(8,128)S(1)}, f32[64,8,128]{2,1,0:T(8,128)}) fusion(f32[64,128]{1,0:T(8,128)S(1)} %get-tuple-element.39, f32[8]{0:T(128)S(1)} %bitcast.90), kind=kLoop, calls=%fused_computation.37 | loop fusion | flops 65536 | bytes 557088 | tf_op jit(solution)/shard_map/cos | solution.py:43
  15.6 1.8 %multiply_cosine_fusion.1 = (f32[64,8,128]{2,1,0:T(8,128)}, f32[64,8,128]{2,1,0:T(8,128)}) fusion(f32[64,128]{1,0:T(8,128)S(1)} %get-tuple-element.40, f32[8]{0:T(128)S(1)} %slice_bitcast_fusion.4), kind=kLoop, calls=%fused_computation.35 | loop fusion | flops 65536 | bytes 557088 | tf_op jit(solution)/shard_map/cos | solution.py:43
  17.4 3.8 %multiply_cosine_fusion = (f32[64,24,128]{2,1,0:T(8,128)}, f32[64,24,128]{2,1,0:T(8,128)}) fusion(f32[64,128]{1,0:T(8,128)S(1)} %get-tuple-element.41, f32[24]{0:T(128)S(1)} %bitcast.89), kind=kLoop, calls=%fused_computation.9 | loop fusion | flops 196608 | bytes 1605728 | tf_op jit(solution)/shard_map/cos | solution.py:43
  21.2 0.6 add_negate_fusion
  21.8 0.5 compare_and_fusion.1
  22.4 0.5 broadcast.336
  22.9 0.7 reduce.11
  23.5 0.1 reshape.325
  23.6 0.6 pad_clamp_fusion
  24.2 0.9 gather_fusion.2
  25.1 2.8 %gather_fusion = f32[128,64,128]{2,1,0:T(8,128)} fusion(f32[64,64,128]{2,1,0:T(8,128)S(1)} %copy-done, s32[1024]{0:T(1024)S(1)} %get-tuple-element.57), kind=kCustom, calls=%fused_computation | custom fusion | bytes 8389120 | tf_op jit(solution)/shard_map/jit(_take)/gather | solution.py:183
  27.9 0.8 copy_select_fusion
  28.7 5.1 %all-to-all-start.2 = ((f32[8,16,3,128]{3,1,2,0:T(8,128)}), f32[8,16,3,128]{3,1,2,0:T(8,128)S(1)}, u32[]{:S(2)}, u32[]{:S(2)}) async-start(f32[8,16,3,128]{3,1,2,0:T(8,128)} %copy_select_fusion), calls=%async_computation.2 | async-start | bytes 393216 | tf_op jit(solution)/shard_map/all_to_all | solution.py:191
  33.8 4.5 %broadcast_select_fusion = f32[8,16,64,128]{3,2,1,0:T(8,128)} fusion(f32[8,16,64,128]{3,2,1,0:T(8,128)} %bitcast.81, pred[8,16]{1,0:T(8,128)(4,1)S(1)} %compare_and_fusion), kind=kLoop, calls=%fused_computation.6 | loop fusion | flops 1048576 | bytes 8388736 | tf_op jit(solution)/shard_map/jit(_take)/select_n | solution.py:183
  38.3 3.8 %all-to-all-done.2 = f32[8,16,3,128]{3,1,2,0:T(8,128)S(1)} async-done(((f32[8,16,3,128]{3,1,2,0:T(8,128)}), f32[8,16,3,128]{3,1,2,0:T(8,128)S(1)}, u32[]{:S(2)}, u32[]{:S(2)}) %all-to-all-start.2) | async-done | bytes 196640 | tf_op jit(solution)/shard_map/all_to_all | solution.py:191
  42.1 0.7 copy-done.4
  42.7 4.6 %all-to-all-start.1 = ((f32[8,16,64,128]{3,2,1,0:T(8,128)}), f32[8,16,64,128]{3,2,1,0:T(8,128)}, u32[]{:S(2)}, u32[]{:S(2)}) async-start(f32[8,16,64,128]{3,2,1,0:T(8,128)} %broadcast_select_fusion), calls=%async_computation.1 | async-start | bytes 8388608 | tf_op jit(solution)/shard_map/all_to_all | solution.py:190
  47.3 1.2 pad_maximum_fusion.1.yz_ref
  48.5 2.6 %copy.34 = f32[64,3,128]{1,2,0:T(8,128)} copy(f32[64,3,128]{2,0,1:T(8,128)S(1)} %copy-done.2) | data formatting | bytes 196608 | tf_op args[0]
  51.2 0.1 copy.35.pos_ref
  52.0 1.5 pad_maximum_fusion.x_ref
  53.6 0.2 fusion.7
  53.9 1.8 %copy-done.1 = f32[64,3,128]{1,2,0:T(8,128)S(1)} copy-done((f32[64,3,128]{1,2,0:T(8,128)S(1)}, f32[64,3,128]{1,2,0:T(8,128)}, u32[]{:S(2)}) %copy-start.1) | copy-done | bytes 98328
  55.8 31.6 %shard_map.120 = f32[64,128]{1,0:T(8,128)S(1)} custom-call(bf16[320,3072]{1,0:T(8,128)(2,1)S(1)} %maximum_dynamic-update-slice_fusion.table_ref, f32[64,64,128]{2,1,0:T(8,128)S(1)} %copy-done, f32[64,48,128]{2,1,0:T(8,128)S(1)} %pad_maximum_fusion.x_ref, f32[64,32,128]{2,1,0:T(8,128)S(1)} %pad_maximum_fusion.1.yz_ref, f32[64,3,128]{2,1,0:T(4,128)S(1)} %copy.35.pos_ref, ...), custom_call_target="tpu_custom_call" | custom-call | flops 32212254720 | bytes 2097152 | tf_op jit(solution)/shard_map/pallas_call | solution.py:120
  87.4 0.1 reduce_sum.50
  87.6 59.7 %all-gather.1 = f32[8,3,64]{2,1,0:T(4,128)S(1)} all-gather(f32[1,3,64]{2,1,0:T(4,128)S(1)} %maximum_bitcast_fusion), channel_id=2, replica_groups=mesh['twist'=4,'walk'=8] {'walk'}, dimensions={0}, use_global_device_ids=true | all-gather | bytes 6912 | tf_op jit(solution)/shard_map/all_gather | solution.py:198
  147.3 0.2 copy.36
  148.1 0.6 fusion.15
  148.7 1.9 %maximum_multiply_fusion = f32[2]{0:T(128)} fusion(f32[1]{0:T(128)} %bitcast.30, f32[1]{0:T(128)} %bitcast.29), kind=kLoop, calls=%fused_computation.89 | loop fusion | flops 4 | bytes 16 | tf_op jit(solution)/shard_map/div | solution.py:199
  150.6 0.7 gather_fusion.4
  151.3 0.1 select_bitcast_fusion
  151.4 0.6 copy.38
  152.1 0.1 copy.33
  152.2 0.7 gather_fusion.3
  152.8 0.2 select_select_fusion.1
  153.0 0.6 copy.37
  153.7 2.9 %gather_fusion.1 = f32[64,64,128]{2,1,0:T(8,128)S(1)} fusion(f32[128,64,128]{2,1,0:T(8,128)} %bitcast.9, s32[1024]{0:T(1024)S(1)} %pad_clamp_fusion.1), kind=kCustom, calls=%fused_computation.1 | custom fusion | bytes 4194560 | tf_op jit(solution)/shard_map/jit(_take)/gather | solution.py:206
  156.6 1.6 %select_select_fusion = f32[64,64,128]{2,1,0:T(8,128)} fusion(f32[64,64,128]{2,1,0:T(8,128)S(1)} %gather_fusion.1, pred[64]{0:T(512)(128)(4,1)S(1)} %get-tuple-element.27, pred[64]{0:T(512)(128)(4,1)S(1)} %iota_compare_fusion.3), kind=kLoop, calls=%fused_computation.5 | loop fusion | flops 1048576 | bytes 4194432 | tf_op jit(solution)/shard_map/jit(_where)/select_n | solution.py:204
  (50 shorter events, 0.3 us)
Async XLA Ops:
  0.6 21.2 %copy-start.12 = (s32[64,1]{0,1:T(1,128)S(1)}, s32[64,1]{0,1:T(1,128)}, u32[]{:S(2)}) copy-start(s32[64,1]{0,1:T(1,128)} %param.15) | copy-start | bytes 772
  0.6 21.2 %copy-start.14 = (s32[64]{0:T(128)S(1)}, s32[64]{0:T(128)}, u32[]{:S(2)}) copy-start(s32[64]{0:T(128)} %param.16) | copy-start | bytes 772
  0.7 23.6 %copy-start.2 = (f32[64,3,128]{2,0,1:T(8,128)S(1)}, f32[64,3,128]{2,0,1:T(8,128)}, u32[]{:S(2)}) copy-start(f32[64,3,128]{2,0,1:T(8,128)} %param.9) | copy-start | bytes 294916
  1.6 2.2 %copy-start.10 = (s32[64]{0:T(128)}, s32[64]{0:T(128)S(1)}, u32[]{:S(2)}) copy-start(s32[64]{0:T(128)S(1)} %convert_reduce_fusion) | copy-start | bytes 772
  3.8 18.6 %all-to-all-start = ((s32[8,1,16]{2,1,0:T(1,128)}), s32[8,1,16]{2,1,0:T(1,128)S(1)}, u32[]{:S(2)}, u32[]{:S(2)}) async-start(s32[8,1,16]{2,1,0:T(1,128)} %bitcast.5), calls=%async_computation | async-start | bytes 8192 | tf_op jit(solution)/shard_map/all_to_all | solution.py:181
  17.4 7.7 %copy-start = (f32[64,64,128]{2,1,0:T(8,128)S(1)}, f32[64,64,128]{2,1,0:T(8,128)}, u32[]{:S(2)}) copy-start(f32[64,64,128]{2,1,0:T(8,128)} %inverse_ref.1) | copy-start | bytes 6291460
  28.7 13.4 %all-to-all-start.2 = ((f32[8,16,3,128]{3,1,2,0:T(8,128)}), f32[8,16,3,128]{3,1,2,0:T(8,128)S(1)}, u32[]{:S(2)}, u32[]{:S(2)}) async-start(f32[8,16,3,128]{3,1,2,0:T(8,128)} %copy_select_fusion), calls=%async_computation.2 | async-start | bytes 393216 | tf_op jit(solution)/shard_map/all_to_all | solution.py:191
  42.1 0.7 copy-start.4
  42.7 111.0 %all-to-all-start.1 = ((f32[8,16,64,128]{3,2,1,0:T(8,128)}), f32[8,16,64,128]{3,2,1,0:T(8,128)}, u32[]{:S(2)}, u32[]{:S(2)}) async-start(f32[8,16,64,128]{3,2,1,0:T(8,128)} %broadcast_select_fusion), calls=%async_computation.1 | async-start | bytes 8388608 | tf_op jit(solution)/shard_map/all_to_all | solution.py:190
  51.1 2.3 %copy-start.6 = (bf16[64,1536]{1,0:T(8,128)(2,1)S(1)}, bf16[64,1536]{1,0:T(8,128)(2,1)}, u32[]{:S(2)}) copy-start(bf16[64,1536]{1,0:T(8,128)(2,1)} %get-tuple-element.37) | copy-start | bytes 589828
  51.2 2.3 %copy-start.7 = (bf16[64,1536]{1,0:T(8,128)(2,1)S(1)}, bf16[64,1536]{1,0:T(8,128)(2,1)}, u32[]{:S(2)}) copy-start(bf16[64,1536]{1,0:T(8,128)(2,1)} %get-tuple-element.38) | copy-start | bytes 589828
  51.2 2.4 %copy-start.3 = (f32[2,64,1536]{2,1,0:T(8,128)S(1)}, f32[2,64,1536]{2,1,0:T(8,128)}, u32[]{:S(2)}) copy-start(f32[2,64,1536]{2,1,0:T(8,128)} %param.11) | copy-start | bytes 2359300
  51.2 2.4 %copy-start.8 = (f32[1536]{0:T(1024)S(1)}, f32[1536]{0:T(1024)}, u32[]{:S(2)}) copy-start(f32[1536]{0:T(1024)} %get-tuple-element.51) | copy-start | bytes 18436
  53.6 2.2 %copy-start.1 = (f32[64,3,128]{1,2,0:T(8,128)S(1)}, f32[64,3,128]{1,2,0:T(8,128)}, u32[]{:S(2)}) copy-start(f32[64,3,128]{1,2,0:T(8,128)} %copy.34) | copy-start | bytes 294916
  55.8 31.8 %copy-start.15 = (s32[64]{0:T(128)S(1)}, s32[64]{0:T(128)}, u32[]{:S(2)}) copy-start(s32[64]{0:T(128)} %param.14) | copy-start | bytes 772
  55.8 94.8 %copy-start.11 = (s32[64]{0:T(128)S(1)}, s32[64]{0:T(128)}, u32[]{:S(2)}) copy-start(s32[64]{0:T(128)} %copy-done.10) | copy-start | bytes 772
  55.8 94.8 %copy-start.13 = (s32[64,1]{0,1:T(1,128)S(1)}, s32[64,1]{0,1:T(1,128)}, u32[]{:S(2)}) copy-start(s32[64,1]{0,1:T(1,128)} %param.15) | copy-start | bytes 772
  55.8 95.6 %copy-start.9 = (pred[64]{0:T(512)(128)(4,1)S(1)}, pred[64]{0:T(512)(128)(4,1)}, u32[]{:S(2)}) copy-start(pred[64]{0:T(512)(128)(4,1)} %get-tuple-element.25) | copy-start | bytes 196
  55.8 96.3 %copy-start.5 = (f32[8,16,3,128]{3,1,2,0:T(8,128)S(1)}, f32[8,16,3,128]{3,1,2,0:T(8,128)}, u32[]{:S(2)}) copy-start(f32[8,16,3,128]{3,1,2,0:T(8,128)} %copy-done.4) | copy-start | bytes 589828

commit v2 on v1

--- a/solution.py
+++ b/solution.py
@@ -155,6 +155,44 @@
     return jnp.sum(jnp.where(matches, wanted[None, None, :], 0), axis=2)
 
 
+def state_kernel(device_ref, rank_ref, live_ref, held_ref, out_ref, sem):
+    slots, rows, _ = out_ref.shape
+
+    def copy(slot):
+        first = pl.multiple_of(rank_ref[slot] * rows, 8)
+        return pltpu.make_async_copy(
+            held_ref.at[device_ref[slot], pl.ds(first, rows)], out_ref.at[slot], sem.at[slot]
+        )
+
+    @pl.loop(0, slots)
+    def _(slot):
+        @pl.when(slot < live_ref[0])
+        def _():
+            copy(slot).start()
+
+        @pl.when(slot >= live_ref[0])
+        def _():
+            out_ref[slot] = jnp.zeros(out_ref.shape[1:], out_ref.dtype)
+
+    @pl.loop(0, slots)
+    def _(slot):
+        @pl.when(slot < live_ref[0])
+        def _():
+            copy(slot).wait()
+
+
+def gather_states(received, device, rank, live_count, rows):
+    slots, electrons = device.shape[0], received.shape[2]
+    smem = pl.BlockSpec(memory_space=pltpu.SMEM)
+    return pl.pallas_call(
+        state_kernel,
+        out_shape=jax.ShapeDtypeStruct((slots, rows, electrons), received.dtype),
+        in_specs=[smem, smem, smem, pl.BlockSpec(memory_space=pl.ANY)],
+        out_specs=pl.BlockSpec(memory_space=pltpu.VMEM),
+        scratch_shapes=[pltpu.SemaphoreType.DMA((slots,))],
+    )(device, rank, live_count, received)
+
+
 def body(
     positions,
     inverse_slater,
@@ -180,37 +218,33 @@
     requests = build_requests(source_device, slot_rank, anchor_slot, peer_count, capacity)
     served = lax.all_to_all(requests, "walk", split_axis=0, concat_axis=0, tiled=True)
     served_flat = served.reshape(peer_count * capacity)
-    send_inverse = jnp.take(inverse_slater, served_flat, axis=0).reshape(
-        peer_count, capacity, orbital_count, electrons
-    )
-    send_positions = jnp.take(positions, served_flat, axis=0).reshape(
-        peer_count, capacity, 3, electrons
-    )
-    recv_inverse, recv_positions = (
-        lax.all_to_all(send_inverse, "walk", split_axis=0, concat_axis=0, tiled=True),
-        lax.all_to_all(send_positions, "walk", split_axis=0, concat_axis=0, tiled=True),
+    send_inverse = jnp.take(inverse_slater, served_flat, axis=0, mode="clip").reshape(
+        peer_count, capacity * orbital_count, electrons
+    )
+    send_positions = jnp.take(positions, served_flat, axis=0, mode="clip").reshape(
+        peer_count, capacity * 3, electrons
+    )
+    send = jnp.concatenate([send_inverse, send_positions], axis=1)
+    received = lax.all_to_all(send, "walk", split_axis=0, concat_axis=0, tiled=True)
+    local_positions, orbitals, twist_angle, send = lax.optimization_barrier(
+        (positions, orbitals, twist_angle, send)
     )
     momenta = wave_momenta(twist_angle, orbitals.shape[2])
     table = build_table(orbitals, momenta)
-    energy = local_energies(table, momenta, inverse_slater, positions)
+    energy = local_energies(table, momenta, inverse_slater, local_positions)
     weight = jnp.exp(-time_step * (energy - trial_energy[0]))
     scaled = multiplicity.astype(jnp.float32) * weight
     shared = lax.all_gather(jnp.stack([weight, energy, scaled]), "walk")
     group_stats = jnp.stack(
         [jnp.sum(shared[:, 2] * shared[:, 1]), jnp.sum(shared[:, 2])]
     ) / (walk_dev * peer_count)
-    target = source_device * capacity + slot_rank
     live_slot = slot_ids < live_count[0]
-    new_inverse = jnp.where(
-        live_slot[:, None, None],
-        jnp.take(
-            recv_inverse.reshape(peer_count * capacity, orbital_count, electrons), target, axis=0
-        ),
-        0.0,
-    )
+    split = capacity * orbital_count
+    tail = received[:, split:].reshape(peer_count * capacity, 3, electrons)
+    new_inverse = gather_states(received, source_device, slot_rank, live_count, orbital_count)
     new_positions = jnp.where(
         live_slot[:, None, None],
-        jnp.take(recv_positions.reshape(peer_count * capacity, 3, electrons), target, axis=0),
+        jnp.take(tail, source_device * capacity + slot_rank, axis=0, mode="clip"),
         0.0,
     )
     source = source_device * walk_dev + anchor_slot

time: 159 us -> 147 us (0.925)
  other arithmetic: 26.4 us -> 17.9 us
  starting transfers between devices: 16 us -> 11 us
  Pallas kernels: 31.6 us -> 36 us
  local copies, waits for them, and re-layouts: 18.3 us -> 14.9 us
    select_n x5 -> x1, other arithmetic: 7.07 us -> 0.13 us  [body(): jnp.where(live_slot[:, None, None], jnp.take(tail, source_device * capaci...]
    all_to_all x2 -> x1, starting transfers between devices: 9.66 us -> 4.68 us  [body(): lax.all_to_all(send, 'walk', split_axis=0, concat_axis=0, tiled=True)]
    concatenate x0 -> x1, other arithmetic: none -> 4.53 us  [body(): send = jnp.concatenate([send_inverse, send_positions], axis=1)]
    pallas_call x0 -> x1, Pallas kernels: none -> 4.41 us  [gather_states(): pl.pallas_call(state_kernel, out_shape=jax.ShapeDtypeStruct((slots, rows,...]
    all_to_all x2 -> x1, waiting for transfers between devices: 3.82 us -> 0.01 us  [body(): lax.all_to_all(send, 'walk', split_axis=0, concat_axis=0, tiled=True)]
    all_to_all x1, waiting for transfers between devices: 0.01 us -> 2.81 us  [body(): lax.all_to_all(requests, 'walk', split_axis=0, concat_axis=0, tiled=True)]
    optimization_barrier x0 -> x2, local copies, waits for them, and re-layouts: none -> 2.72 us  [body(): lax.optimization_barrier((positions, orbitals, twist_angle, send))]
    cos x3, other arithmetic: 7.35 us -> 4.75 us  [axis_waves(): return jnp.concatenate([jnp.cos(angle), jnp.sin(angle)], axis=1)]
  transfers between devices with their start and end apart: 3 -> 2, of which waited for: 1 -> 1; matrix products, arithmetic and copies ran while one was open for 18% -> 10% of each run, Pallas kernels for 20% -> 22%
where the time goes in v2:
time: 147 us; the launch traced here: 146 us
  blocking collectives  61 us (41%)
  Pallas kernels  36 us (24%)
  other arithmetic  17.9 us (12%)
  local copies, waits for them, and re-layouts  14.9 us (10%)
  starting transfers between devices  11 us (7%)
  waiting for transfers between devices  2.81 us (2%)
  between operations  2.24 us (2%)
    all_gather x1, blocking collectives, body(): shared = lax.all_gather(jnp.stack([weight, energy, scaled]), 'walk')  61 us
    pallas_call x1, Pallas kernels, local_energies(): pl.pallas_call(energy_kernel, out_shape=jax.ShapeDtypeStruct((walkers, el...  31.6 us
    all_to_all x1, starting transfers between devices, body(): lax.all_to_all(requests, 'walk', split_axis=0, concat_axis=0, tiled=True)  6.35 us
    cos x3, other arithmetic, axis_waves(): return jnp.concatenate([jnp.cos(angle), jnp.sin(angle)], axis=1)  4.75 us
    all_to_all x1, starting transfers between devices, body(): lax.all_to_all(send, 'walk', split_axis=0, concat_axis=0, tiled=True)  4.68 us
    concatenate x1, other arithmetic, body(): send = jnp.concatenate([send_inverse, send_positions], axis=1)  4.53 us
    pallas_call x1, Pallas kernels, gather_states(): pl.pallas_call(state_kernel, out_shape=jax.ShapeDtypeStruct((slots, rows,...  4.41 us
    unnamed x16, local copies, waits for them, and re-layouts  4.11 us
  transfers between devices with their start and end apart: 2, of which 1 were waited for; matrix products, arithmetic and copies ran while one was open for 10% of the time, Pallas kernels for 22%

profile of v2, /device:TPU:0, one launch (start us, length us, event | category | flops | bytes accessed | tf_op | source)
XLA Modules:
  0.0 146.0 jit_solution(17999348983753448625)
XLA Ops:
  0.6 1.0 convert_reduce_fusion.rank_ref
  1.6 0.0 copy-start.4
  1.7 0.7 iota_compare_fusion.2
  2.3 1.5 %select_reduce_fusion = s32[8,16]{1,0:T(8,128)} fusion(s32[64]{0:T(128)} %param.16, pred[16,64]{1,0:T(8,128)(4,1)S(1)} %iota_compare_fusion.1, pred[8,64]{1,0:T(8,128)(4,1)S(1)} %iota_compare_fusion.2), kind=kLoop, calls=%fused_computation.37 | loop fusion | flops 24448 | bytes 2304 | tf_op jit(solution)/shard_map/reduce_sum | solution.py:155
  3.8 6.4 %all-to-all-start = ((s32[8,1,16]{2,1,0:T(1,128)}), s32[8,1,16]{2,1,0:T(1,128)S(1)}, u32[]{:S(2)}, u32[]{:S(2)}) async-start(s32[8,1,16]{2,1,0:T(1,128)} %bitcast.2), calls=%async_computation | async-start | bytes 8192 | tf_op jit(solution)/shard_map/all_to_all | solution.py:219
  10.1 0.7 compare_and_fusion
  10.8 0.7 fusion.16
  12.8 2.8 %all-to-all-done = s32[8,1,16]{2,1,0:T(1,128)S(1)} async-done(((s32[8,1,16]{2,1,0:T(1,128)}), s32[8,1,16]{2,1,0:T(1,128)S(1)}, u32[]{:S(2)}, u32[]{:S(2)}) %all-to-all-start) | async-done | bytes 544 | tf_op jit(solution)/shard_map/all_to_all | solution.py:219
  15.7 0.5 broadcast.293
  16.2 0.7 reduce.11
  16.8 0.1 reshape.283
  16.9 1.8 %gather_fusion.1 = f32[128,3,128]{2,0,1:T(8,128)S(1)} fusion(f32[64,3,128]{2,0,1:T(8,128)} %param.9, s32[1024]{0:T(1024)S(1)} %get-tuple-element.59), kind=kCustom, calls=%fused_computation.1 | custom fusion | bytes 393728 | tf_op jit(solution)/shard_map/jit(_take)/gather | solution.py:224
  18.7 0.1 copy.32
  18.8 0.1 reshape.278
  18.9 2.7 %gather_fusion = f32[128,64,128]{2,1,0:T(8,128)} fusion(f32[64,64,128]{2,1,0:T(8,128)S(1)} %copy-done, s32[1024]{0:T(1024)S(1)} %get-tuple-element.59), kind=kCustom, calls=%fused_computation | custom fusion | bytes 8389120 | tf_op jit(solution)/shard_map/jit(_take)/gather | solution.py:221
  21.7 4.5 %pad_maximum_fusion = f32[8,1072,128]{2,1,0:T(8,128)} fusion(f32[8,48,128]{2,1,0:T(8,128)S(1)} %reshape.278, f32[8,1024,128]{2,1,0:T(8,128)} %bitcast.73), kind=kLoop, calls=%fused_computation.4 | loop fusion | flops 1097728 | bytes 8781824 | tf_op jit(solution)/shard_map/concatenate | solution.py:227
  26.2 4.7 %all-to-all-start.1 = ((f32[8,1072,128]{2,1,0:T(8,128)}), f32[8,1072,128]{2,1,0:T(8,128)}, u32[]{:S(2)}, u32[]{:S(2)}) async-start(f32[8,1072,128]{2,1,0:T(8,128)} %pad_maximum_fusion), calls=%async_computation.1 | async-start | bytes 8781824 | tf_op jit(solution)/shard_map/all_to_all | solution.py:228
  30.9 0.1 fusion.10
  31.0 0.1 slice.58
  31.1 0.1 slice.60
  31.2 0.1 copy.34.pos_ref
  31.3 2.7 %copy.33 = f32[64,3,128]{1,2,0:T(8,128)} copy(f32[64,3,128]{2,0,1:T(8,128)S(1)} %copy-done.2) | data formatting | bytes 196608 | tf_op jit(solution)/shard_map/optimization_barrier | solution.py:229
  34.0 1.0 multiply_cosine_fusion.1
  35.0 1.0 multiply_cosine_fusion.2
  35.9 0.1 pad_maximum_fusion.2.yz_ref
  36.0 0.1 slice_reduce_fusion
  36.1 2.8 %multiply_cosine_fusion = (f32[64,24,128]{2,1,0:T(8,128)S(1)}, f32[64,24,128]{2,1,0:T(8,128)S(1)}) fusion(f32[64,128]{1,0:T(8,128)S(1)} %get-tuple-element.45, f32[24]{0:T(128)S(1)} %bitcast.78), kind=kLoop, calls=%fused_computation.7 | loop fusion | flops 196608 | bytes 1605728 | tf_op jit(solution)/shard_map/cos | solution.py:43
  38.9 0.0 copy-start.3
  38.9 0.1 pad_maximum_fusion.1.x_ref
  39.0 1.0 copy-done.3
  40.1 0.2 fusion.7
  40.5 1.8 %copy-done.1 = f32[64,3,128]{1,2,0:T(8,128)S(1)} copy-done((f32[64,3,128]{1,2,0:T(8,128)S(1)}, f32[64,3,128]{1,2,0:T(8,128)}, u32[]{:S(2)}) %copy-start.1) | copy-done | bytes 98328
  42.3 31.6 %shard_map.121 = f32[64,128]{1,0:T(8,128)S(1)} custom-call(bf16[320,3072]{1,0:T(8,128)(2,1)S(1)} %maximum_dynamic-update-slice_fusion.table_ref, f32[64,64,128]{2,1,0:T(8,128)S(1)} %copy-done, f32[64,48,128]{2,1,0:T(8,128)S(1)} %pad_maximum_fusion.1.x_ref, f32[64,32,128]{2,1,0:T(8,128)S(1)} %pad_maximum_fusion.2.yz_ref, f32[64,3,128]{2,1,0:T(4,128)S(1)} %copy.34.pos_ref, ...), custom_call_target="tpu_custom_call" | custom-call | flops 32212254720 | bytes 2097152 | tf_op jit(solution)/shard_map/pallas_call | solution.py:120
  73.9 0.1 reduce_sum.50
  74.1 61.0 %all-gather.1 = f32[8,3,64]{2,1,0:T(4,128)S(1)} all-gather(f32[1,3,64]{2,1,0:T(4,128)S(1)} %maximum_bitcast_fusion), channel_id=2, replica_groups=mesh['twist'=4,'walk'=8] {'walk'}, dimensions={0}, use_global_device_ids=true | all-gather | bytes 6912 | tf_op jit(solution)/shard_map/all_gather | solution.py:237
  135.1 0.2 copy.35
  135.2 0.6 gather_fusion.3
  135.8 0.1 select_bitcast_fusion
  135.9 0.6 copy.37
  136.6 0.6 fusion.15
  137.2 1.9 %maximum_multiply_fusion = f32[2]{0:T(128)} fusion(f32[1]{0:T(128)} %bitcast.24, f32[1]{0:T(128)} %bitcast.23), kind=kLoop, calls=%fused_computation.80 | loop fusion | flops 4 | bytes 16 | tf_op jit(solution)/shard_map/div | solution.py:238
  139.1 0.0 all-to-all-done.1.held_ref
  139.1 0.9 slice.75
  140.0 0.1 reshape.279
  140.1 0.7 gather_fusion.2
  140.8 0.1 broadcast_select_fusion
  140.9 0.6 copy.36
  141.5 4.4 %shard_map.120 = f32[64,64,128]{2,1,0:T(8,128)} custom-call(s32[64]{0:T(128)} %bitcast.77, s32[64]{0:T(128)} %copy-done.4, s32[1]{0:T(128)} %copy.43.live_ref, f32[8,1072,128]{2,1,0:T(8,128)} %all-to-all-done.1.held_ref), custom_call_target="tpu_custom_call" | custom-call | tf_op jit(solution)/shard_map/pallas_call | solution.py:187
  (29 shorter events, 0.3 us)
Async XLA Ops:
  0.6 18.3 %copy-start = (f32[64,64,128]{2,1,0:T(8,128)S(1)}, f32[64,64,128]{2,1,0:T(8,128)}, u32[]{:S(2)}) copy-start(f32[64,64,128]{2,1,0:T(8,128)} %inverse_ref.1) | copy-start | bytes 6291460
  1.6 20.0 %copy-start.4 = (s32[64]{0:T(128)}, s32[64]{0:T(128)S(1)}, u32[]{:S(2)}) copy-start(s32[64]{0:T(128)S(1)} %convert_reduce_fusion.rank_ref) | copy-start | bytes 772
  3.8 11.9 %all-to-all-start = ((s32[8,1,16]{2,1,0:T(1,128)}), s32[8,1,16]{2,1,0:T(1,128)S(1)}, u32[]{:S(2)}, u32[]{:S(2)}) async-start(s32[8,1,16]{2,1,0:T(1,128)} %bitcast.2), calls=%async_computation | async-start | bytes 8192 | tf_op jit(solution)/shard_map/all_to_all | solution.py:219
  26.2 4.7 %copy-start.5 = (f32[3]{0:T(128)S(1)}, f32[3]{0:T(128)}, u32[]{:S(2)}) copy-start(f32[3]{0:T(128)} %param.12) | copy-start | bytes 40
  26.2 5.0 %copy-start.2 = (f32[64,3,128]{2,0,1:T(8,128)S(1)}, f32[64,3,128]{2,0,1:T(8,128)}, u32[]{:S(2)}) copy-start(f32[64,3,128]{2,0,1:T(8,128)} %param.9) | copy-start | bytes 294916
  26.2 112.8 %all-to-all-start.1 = ((f32[8,1072,128]{2,1,0:T(8,128)}), f32[8,1072,128]{2,1,0:T(8,128)}, u32[]{:S(2)}, u32[]{:S(2)}) async-start(f32[8,1072,128]{2,1,0:T(8,128)} %pad_maximum_fusion), calls=%async_computation.1 | async-start | bytes 8781824 | tf_op jit(solution)/shard_map/all_to_all | solution.py:228
  38.9 1.1 copy-start.3
  40.1 2.2 %copy-start.1 = (f32[64,3,128]{1,2,0:T(8,128)S(1)}, f32[64,3,128]{1,2,0:T(8,128)}, u32[]{:S(2)}) copy-start(f32[64,3,128]{1,2,0:T(8,128)} %copy.33) | copy-start | bytes 294916
  42.3 31.8 %copy-start.6 = (s32[64]{0:T(128)S(1)}, s32[64]{0:T(128)}, u32[]{:S(2)}) copy-start(s32[64]{0:T(128)} %param.14) | copy-start | bytes 772

commit v3 on v2

--- a/solution.py
+++ b/solution.py
@@ -193,6 +193,48 @@
     )(device, rank, live_count, received)
 
 
+def pack_kernel(capacity, served_ref, held_ref, tail_ref, out_ref, sem):
+    peers = out_ref.shape[0]
+    rows = held_ref.shape[1]
+
+    def copy(peer, room):
+        slot = peer * capacity + room
+        first = pl.multiple_of(room * rows, 8)
+        return pltpu.make_async_copy(
+            held_ref.at[served_ref[slot]], out_ref.at[peer, pl.ds(first, rows)], sem.at[slot]
+        )
+
+    @pl.loop(0, peers)
+    def _(peer):
+        for room in range(capacity):
+            copy(peer, room).start()
+
+    out_ref[:, capacity * rows :, :] = tail_ref[...]
+
+    @pl.loop(0, peers)
+    def _(peer):
+        for room in range(capacity):
+            copy(peer, room).wait()
+
+
+def pack_states(held, served, tail):
+    peers, extra, electrons = tail.shape
+    capacity = served.shape[0] // peers
+    return pl.pallas_call(
+        lambda *refs: pack_kernel(capacity, *refs),
+        out_shape=jax.ShapeDtypeStruct(
+            (peers, capacity * held.shape[1] + extra, electrons), held.dtype
+        ),
+        in_specs=[
+            pl.BlockSpec(memory_space=pltpu.SMEM),
+            pl.BlockSpec(memory_space=pl.ANY),
+            pl.BlockSpec(memory_space=pltpu.VMEM),
+        ],
+        out_specs=pl.BlockSpec(memory_space=pltpu.VMEM),
+        scratch_shapes=[pltpu.SemaphoreType.DMA((peers * capacity,))],
+    )(served, held, tail)
+
+
 def body(
     positions,
     inverse_slater,
@@ -218,13 +260,10 @@
     requests = build_requests(source_device, slot_rank, anchor_slot, peer_count, capacity)
     served = lax.all_to_all(requests, "walk", split_axis=0, concat_axis=0, tiled=True)
     served_flat = served.reshape(peer_count * capacity)
-    send_inverse = jnp.take(inverse_slater, served_flat, axis=0, mode="clip").reshape(
-        peer_count, capacity * orbital_count, electrons
-    )
     send_positions = jnp.take(positions, served_flat, axis=0, mode="clip").reshape(
         peer_count, capacity * 3, electrons
     )
-    send = jnp.concatenate([send_inverse, send_positions], axis=1)
+    send = pack_states(inverse_slater, served_flat, send_positions)
     received = lax.all_to_all(send, "walk", split_axis=0, concat_axis=0, tiled=True)
     local_positions, orbitals, twist_angle, send = lax.optimization_barrier(
         (positions, orbitals, twist_angle, send)

time: 147 us -> 148 us (level)
  Pallas kernels: 36 us -> 43.3 us
  other arithmetic: 17.9 us -> 13.3 us
  local copies, waits for them, and re-layouts: 14.9 us -> 13.4 us
    pallas_call x0 -> x1, Pallas kernels: none -> 7.2 us  [pack_states(): pl.pallas_call(lambda *refs: pack_kernel(capacity, *refs), out_shape=jax....]
    concatenate x1 -> x0, other arithmetic: 4.53 us -> none  [body(): send = jnp.concatenate([send_inverse, send_positions], axis=1)]
    gather x1 -> x0, local copies, waits for them, and re-layouts: 2.74 us -> none  [body(): jnp.take(inverse_slater, served_flat, axis=0, mode='clip')]
    unnamed x16 -> x18, local copies, waits for them, and re-layouts: 4.11 us -> 4.72 us
  transfers between devices with their start and end apart: 2 -> 2, of which waited for: 1 -> 1; matrix products, arithmetic and copies ran while one was open for 10% -> 9% of each run, Pallas kernels for 22% -> 22%
where the time goes in v3:
time: 148 us; the launch traced here: 147 us
  blocking collectives  60.6 us (41%)
  Pallas kernels  43.3 us (29%)
  local copies, waits for them, and re-layouts  13.4 us (9%)
  other arithmetic  13.3 us (9%)
  starting transfers between devices  11 us (7%)
  waiting for transfers between devices  2.81 us (2%)
  between operations  2.25 us (2%)
    all_gather x1, blocking collectives, body(): shared = lax.all_gather(jnp.stack([weight, energy, scaled]), 'walk')  60.6 us
    pallas_call x1, Pallas kernels, local_energies(): pl.pallas_call(energy_kernel, out_shape=jax.ShapeDtypeStruct((walkers, el...  31.6 us
    pallas_call x1, Pallas kernels, pack_states(): pl.pallas_call(lambda *refs: pack_kernel(capacity, *refs), out_shape=jax....  7.2 us
    all_to_all x1, starting transfers between devices, body(): lax.all_to_all(requests, 'walk', split_axis=0, concat_axis=0, tiled=True)  6.35 us
    cos x3, other arithmetic, axis_waves(): return jnp.concatenate([jnp.cos(angle), jnp.sin(angle)], axis=1)  4.75 us
    unnamed x18, local copies, waits for them, and re-layouts  4.72 us
    all_to_all x1, starting transfers between devices, body(): lax.all_to_all(send, 'walk', split_axis=0, concat_axis=0, tiled=True)  4.7 us
    pallas_call x1, Pallas kernels, gather_states(): pl.pallas_call(state_kernel, out_shape=jax.ShapeDtypeStruct((slots, rows,...  4.44 us
  transfers between devices with their start and end apart: 2, of which 1 were waited for; matrix products, arithmetic and copies ran while one was open for 9% of the time, Pallas kernels for 22%

profile of v3, /device:TPU:0, one launch (start us, length us, event | category | flops | bytes accessed | tf_op | source)
XLA Modules:
  0.0 146.7 jit_solution(5012613124925627233)
XLA Ops:
  0.6 0.9 convert_reduce_fusion.rank_ref
  1.6 0.7 iota_compare_fusion.2
  2.2 1.5 select_reduce_fusion
  3.7 6.4 %all-to-all-start = ((s32[8,1,16]{2,1,0:T(1,128)}), s32[8,1,16]{2,1,0:T(1,128)S(1)}, u32[]{:S(2)}, u32[]{:S(2)}) async-start(s32[8,1,16]{2,1,0:T(1,128)} %bitcast.2), calls=%async_computation | async-start | bytes 8192 | tf_op jit(solution)/shard_map/all_to_all | solution.py:261
  10.0 0.7 compare_and_fusion
  10.7 0.7 fusion.16
  12.7 2.8 %all-to-all-done = s32[8,1,16]{2,1,0:T(1,128)S(1)} async-done(((s32[8,1,16]{2,1,0:T(1,128)}), s32[8,1,16]{2,1,0:T(1,128)S(1)}, u32[]{:S(2)}, u32[]{:S(2)}) %all-to-all-start) | async-done | bytes 544 | tf_op jit(solution)/shard_map/all_to_all | solution.py:261
  15.6 0.5 broadcast.291
  16.1 0.7 reduce.11
  16.7 0.1 reshape.277.refs_0_
  16.8 1.8 %gather_fusion = f32[128,3,128]{2,0,1:T(8,128)S(1)} fusion(f32[64,3,128]{2,0,1:T(8,128)} %param.9, s32[1024]{0:T(1024)S(1)} %get-tuple-element.59), kind=kCustom, calls=%fused_computation | custom fusion | bytes 393728 | tf_op jit(solution)/shard_map/jit(_take)/gather | solution.py:263
  18.6 0.1 copy.32
  18.7 0.8 reshape.278.refs_2_
  19.5 7.2 %shard_map.120 = f32[8,1072,128]{2,1,0:T(8,128)} custom-call(s32[128]{0:T(128)} %copy-done.4, f32[64,64,128]{2,1,0:T(8,128)} %inverse_ref.1, f32[8,48,128]{2,1,0:T(8,128)} %reshape.278.refs_2_), custom_call_target="tpu_custom_call" | custom-call | tf_op jit(solution)/shard_map/pallas_call | solution.py:223
  26.7 0.0 copy-start.6
  26.7 0.0 copy-start.2
  26.7 4.7 %all-to-all-start.1 = ((f32[8,1072,128]{2,1,0:T(8,128)}), f32[8,1072,128]{2,1,0:T(8,128)}, u32[]{:S(2)}, u32[]{:S(2)}) async-start(f32[8,1072,128]{2,1,0:T(8,128)} %shard_map.120), calls=%async_computation.1 | async-start | bytes 8781824 | tf_op jit(solution)/shard_map/all_to_all | solution.py:267
  31.5 0.1 fusion.10
  31.5 0.1 slice.58
  31.7 0.1 slice.60
  31.8 0.1 copy.34.pos_ref
  31.8 2.7 %copy.33 = f32[64,3,128]{1,2,0:T(8,128)} copy(f32[64,3,128]{2,0,1:T(8,128)S(1)} %copy-done.2) | data formatting | bytes 196608 | tf_op jit(solution)/shard_map/optimization_barrier | solution.py:268
  34.5 1.0 multiply_cosine_fusion.1
  35.5 1.0 multiply_cosine_fusion.2
  36.5 0.1 pad_maximum_fusion.1.yz_ref
  36.6 0.1 slice_reduce_fusion
  36.6 2.8 %multiply_cosine_fusion = (f32[64,24,128]{2,1,0:T(8,128)S(1)}, f32[64,24,128]{2,1,0:T(8,128)S(1)}) fusion(f32[64,128]{1,0:T(8,128)S(1)} %get-tuple-element.45, f32[24]{0:T(128)S(1)} %bitcast.76), kind=kLoop, calls=%fused_computation.5 | loop fusion | flops 196608 | bytes 1605728 | tf_op jit(solution)/shard_map/cos | solution.py:43
  39.4 0.0 copy-start.3
  39.4 0.1 pad_maximum_fusion.x_ref
  39.6 1.0 copy-done.3
  40.6 0.2 fusion.7
  41.0 1.2 copy-done.1
  42.2 1.2 copy-done
  43.4 31.6 %shard_map.122 = f32[64,128]{1,0:T(8,128)S(1)} custom-call(bf16[320,3072]{1,0:T(8,128)(2,1)S(1)} %maximum_dynamic-update-slice_fusion.table_ref, f32[64,64,128]{2,1,0:T(8,128)S(1)} %copy-done.1, f32[64,48,128]{2,1,0:T(8,128)S(1)} %pad_maximum_fusion.x_ref, f32[64,32,128]{2,1,0:T(8,128)S(1)} %pad_maximum_fusion.1.yz_ref, f32[64,3,128]{2,1,0:T(4,128)S(1)} %copy.34.pos_ref, ...), custom_call_target="tpu_custom_call" | custom-call | flops 32212254720 | bytes 2097152 | tf_op jit(solution)/shard_map/pallas_call | solution.py:120
  75.1 0.1 reduce_sum.50
  75.2 60.6 %all-gather.1 = f32[8,3,64]{2,1,0:T(4,128)S(1)} all-gather(f32[1,3,64]{2,1,0:T(4,128)S(1)} %maximum_bitcast_fusion), channel_id=2, replica_groups=mesh['twist'=4,'walk'=8] {'walk'}, dimensions={0}, use_global_device_ids=true | all-gather | bytes 6912 | tf_op jit(solution)/shard_map/all_gather | solution.py:276
  135.8 0.2 copy.35
  135.9 0.6 gather_fusion.2
  136.6 0.1 select_bitcast_fusion
  136.6 0.6 copy.37
  137.3 0.6 fusion.15
  137.9 1.9 %maximum_multiply_fusion = f32[2]{0:T(128)} fusion(f32[1]{0:T(128)} %bitcast.23, f32[1]{0:T(128)} %bitcast.22), kind=kLoop, calls=%fused_computation.78 | loop fusion | flops 4 | bytes 16 | tf_op jit(solution)/shard_map/div | solution.py:277
  139.8 0.9 slice.73
  140.7 0.1 reshape.279
  140.8 0.7 gather_fusion.1
  141.5 0.1 broadcast_select_fusion
  141.6 0.6 copy.36
  142.3 4.4 %shard_map.121 = f32[64,64,128]{2,1,0:T(8,128)} custom-call(s32[64]{0:T(128)} %bitcast.75, s32[64]{0:T(128)} %copy-done.5, s32[1]{0:T(128)} %copy.43.live_ref, f32[8,1072,128]{2,1,0:T(8,128)} %all-to-all-done.1.held_ref), custom_call_target="tpu_custom_call" | custom-call | tf_op jit(solution)/shard_map/pallas_call | solution.py:187
  (30 shorter events, 0.3 us)
Async XLA Ops:
  1.5 25.2 %copy-start.5 = (s32[64]{0:T(128)}, s32[64]{0:T(128)S(1)}, u32[]{:S(2)}) copy-start(s32[64]{0:T(128)S(1)} %convert_reduce_fusion.rank_ref) | copy-start | bytes 772
  3.7 11.9 %all-to-all-start = ((s32[8,1,16]{2,1,0:T(1,128)}), s32[8,1,16]{2,1,0:T(1,128)S(1)}, u32[]{:S(2)}, u32[]{:S(2)}) async-start(s32[8,1,16]{2,1,0:T(1,128)} %bitcast.2), calls=%async_computation | async-start | bytes 8192 | tf_op jit(solution)/shard_map/all_to_all | solution.py:261
  16.8 2.7 %copy-start.4 = (s32[128]{0:T(128)}, s32[128]{0:T(128)S(1)}, u32[]{:S(2)}) copy-start(s32[128]{0:T(128)S(1)} %reshape.277.refs_0_) | copy-start | bytes 1540
  26.7 4.7 %copy-start.6 = (f32[3]{0:T(128)S(1)}, f32[3]{0:T(128)}, u32[]{:S(2)}) copy-start(f32[3]{0:T(128)} %param.12) | copy-start | bytes 40
  26.7 5.0 %copy-start.2 = (f32[64,3,128]{2,0,1:T(8,128)S(1)}, f32[64,3,128]{2,0,1:T(8,128)}, u32[]{:S(2)}) copy-start(f32[64,3,128]{2,0,1:T(8,128)} %param.9) | copy-start | bytes 294916
  26.7 113.0 %all-to-all-start.1 = ((f32[8,1072,128]{2,1,0:T(8,128)}), f32[8,1072,128]{2,1,0:T(8,128)}, u32[]{:S(2)}, u32[]{:S(2)}) async-start(f32[8,1072,128]{2,1,0:T(8,128)} %shard_map.120), calls=%async_computation.1 | async-start | bytes 8781824 | tf_op jit(solution)/shard_map/all_to_all | solution.py:267
  39.4 1.1 copy-start.3
  40.6 1.6 %copy-start.1 = (f32[64,64,128]{2,1,0:T(8,128)S(1)}, f32[64,64,128]{2,1,0:T(8,128)}, u32[]{:S(2)}) copy-start(f32[64,64,128]{2,1,0:T(8,128)} %inverse_ref.1) | copy-start | bytes 6291460
  40.6 2.8 %copy-start = (f32[64,3,128]{1,2,0:T(8,128)S(1)}, f32[64,3,128]{1,2,0:T(8,128)}, u32[]{:S(2)}) copy-start(f32[64,3,128]{1,2,0:T(8,128)} %copy.33) | copy-start | bytes 294916
  43.4 31.8 %copy-start.7 = (s32[64]{0:T(128)S(1)}, s32[64]{0:T(128)}, u32[]{:S(2)}) copy-start(s32[64]{0:T(128)} %param.14) | copy-start | bytes 772
